TPU v7x, 32 devices: a whole 2x2x4 slice. The times are simulated.
32 devices in a mesh: mrow: 2 (over y), pcol: 16 (over z, x, core).
Axes of the slice: x: 2, y: 2, z: 4, core: 2. Of those that a mesh axis runs over, the one named last changes fastest.
Arguments:
- snapshots: bfloat16 [7424, 4096], P('mrow', 'pcol'), may hold values from -16 to 16
- area_weight: float32 [4096], P('pcol'), may hold values from 0.2 to 1
Outputs:
- gram_tiles: float32 [2, 16, 1722368], P('mrow', 'pcol')
All inputs are finite; a program needn't handle non-finite values.
Results may differ from a plain program's by a relative error of at most 0.0003.
Values may be sent and summed in bfloat16 or wider, within the bound.
A program may use at most 128 MiB of HBM per device.

v0:
```python
import functools

import jax
import jax.numpy as jnp
from jax import lax
from jax.experimental import pallas as pl
from jax.experimental.pallas import tpu as pltpu
from jax.sharding import PartitionSpec as P

MEMBERS = 7424
MAX_CHUNKS = 8
MESH = pl.DeviceIdType.MESH


def gather_gram(
    n_row, n_col, chunks, early, pieces, tile, x_ref, weight_ref, out_ref, full, cols, sums, recv, send, col_recv, col_send,
    sum_recv, sum_send,
):
    rows, depth = x_ref.shape
    length = n_col // 4
    size = rows // chunks
    span = cols.shape[1]
    i = lax.axis_index("mrow")
    me = lax.axis_index("pcol")
    core = lax.rem(me, 2)
    side = lax.rem(me // 2, 2)
    line = me // 4
    ratio = n_col // n_row
    root = me // ratio
    offset = lax.rem(me, ratio) * tile
    aligned = pl.multiple_of(offset // 16 * 16, 16)
    my_chunk = (aligned + span - 1) // size
    stride = chunks // pieces

    def index(where, which, own):
        return (where * 2 + which) * 2 + own

    up, down = index(line + 1, side, core), index(line - 1, side, core)
    across, sibling = index(line, 1 - side, core), index(line, side, 1 - core)
    has_up, has_down = line + 1 < length, line >= 1
    peers = [lax.rem(i + step, n_row) for step in range(1, n_row)]
    owns_cols = root == i

    barrier = pltpu.get_barrier_semaphore()

    def greet(row, col):
        pl.semaphore_signal(barrier, inc=1, device_id=(row, col), device_id_type=MESH)

    pl.when(has_up)(lambda: greet(i, up))
    pl.when(has_down)(lambda: greet(i, down))
    greet(i, across)
    greet(i, sibling)
    for peer in peers:
        greet(peer, me)

    def add_up(k, total):
        block = x_ref[pl.ds(pl.multiple_of(k * size, 16), size), :].astype(jnp.float32)
        return total + jnp.sum(block.reshape(size // 8, 8, depth), axis=0)

    sums[i] = lax.fori_loop(0, chunks, add_up, jnp.zeros((8, depth), jnp.float32))
    pl.semaphore_wait(barrier, 2 + len(peers) + has_up.astype(jnp.int32) + has_down.astype(jnp.int32))

    def part(s, k):
        return full.at[s, pl.ds(pl.multiple_of(k * size, 16), size)]

    def copy(s, k, way, target):
        return pltpu.make_async_remote_copy(
            src_ref=part(s, k), dst_ref=part(s, k), send_sem=send.at[way, s], recv_sem=recv.at[s, k],
            device_id=(i, target), device_id_type=MESH,
        )

    def col_copy(s, n):
        return pltpu.make_async_remote_copy(
            src_ref=full.at[s, pl.ds(aligned, span)], dst_ref=cols.at[s], send_sem=col_send.at[n],
            recv_sem=col_recv.at[s], device_id=(peers[n], me), device_id_type=MESH,
        )

    def arrived(s, k):
        pltpu.make_async_copy(part(s, k), part(s, k), recv.at[s, k]).wait()

    def share(s, k):
        copy(s, k, 3, sibling).start()

    def to_peers(s, k):
        @pl.when(jnp.logical_and(owns_cols, k == my_chunk))
        def _():
            for n in range(len(peers)):
                col_copy(s, n).start()

    def go_up(s, k):
        pl.when(has_up)(lambda: copy(s, k, 0, up).start())

    def go_down(s, k):
        pl.when(has_down)(lambda: copy(s, k, 1, down).start())

    def sum_copy(n):
        return pltpu.make_async_remote_copy(
            src_ref=sums.at[i], dst_ref=sums.at[i], send_sem=sum_send.at[n], recv_sem=sum_recv.at[i],
            device_id=(peers[n], me), device_id_type=MESH,
        )

    for n in range(len(peers)):
        sum_copy(n).start()
    out_ref[...] = jnp.zeros_like(out_ref)
    for peer in peers:
        pltpu.make_async_copy(sums.at[peer], sums.at[peer], sum_recv.at[peer]).wait()
    mean = jnp.sum(jnp.sum(sums[...], axis=0), axis=0, keepdims=True) / MEMBERS
    root_weight = jnp.sqrt(weight_ref[...])

    def center(k):
        row = pl.ds(pl.multiple_of(k * size, 16), size)
        full[me, row, :] = ((x_ref[row, :].astype(jnp.float32) - mean) * root_weight).astype(jnp.bfloat16)

    def own(k, _):
        pl.when(k + 1 < chunks)(lambda: center(k + 1))
        copy(me, k, 2, across).start()
        go_up(me, k)
        go_down(me, k)
        share(me, k)
        to_peers(me, k)
        return 0

    center(0)
    lax.fori_loop(0, chunks, own, 0)

    def cross_first(k, _):
        arrived(across, k)
        go_up(across, k)
        go_down(across, k)
        share(across, k)
        to_peers(across, k)
        return 0

    lax.fori_loop(0, early, cross_first, 0)

    def valid(sign, distance):
        place = line + sign * distance
        inside = jnp.logical_and(place >= 0, place < length)
        far = distance >= 1 if sign > 0 else distance >= 0
        return jnp.logical_and(inside, far)

    def step(d, _):
        def from_sibling(k):
            for sign in (-1, 1):
                for which, distance in ((side, d), (1 - side, d - 1)):
                    @pl.when(valid(sign, distance))
                    def _():
                        s = index(line + sign * distance, which, 1 - core)
                        arrived(s, k)
                        to_peers(s, k)

        def piece(k, _):
            for sign, forward in ((-1, go_up), (1, go_down)):
                @pl.when(valid(sign, d))
                def _():
                    s = index(line + sign * d, side, core)
                    arrived(s, k)
                    forward(s, k)
                    pl.when(k >= early)(lambda: copy(s, k, 2, across).start())
                    share(s, k)
                    to_peers(s, k)

                    @pl.when(k < early)
                    def _():
                        t = index(line + sign * d, 1 - side, core)
                        arrived(t, k)
                        forward(t, k)
                        share(t, k)
                        to_peers(t, k)

            for sign in (-1, 1):
                @pl.when(jnp.logical_and(valid(sign, d - 1), k >= early))
                def _():
                    s = index(line + sign * (d - 1), 1 - side, core)
                    arrived(s, k)
                    share(s, k)
                    to_peers(s, k)

            pl.when(k >= 1)(lambda: from_sibling(k - 1))

            @pl.when(jnp.logical_and(lax.rem(k, stride) == stride - 1, k // stride < pieces))
            def _():
                multiply(d - 1, k // stride)

            return 0

        lax.fori_loop(0, chunks, piece, 0)
        from_sibling(chunks - 1)
        for sign in (-1, 1):
            for which, distance in ((side, d), (1 - side, d - 1)):
                for other in (core, 1 - core):
                    pl.when(valid(sign, distance))(
                        lambda: take_cols(index(line + sign * distance, which, other))
                    )
        return 0

    def take_cols(s):
        @pl.when(owns_cols)
        def _():
            cols[s] = full[s, pl.ds(aligned, span), :]

        @pl.when(jnp.logical_not(owns_cols))
        def _():
            pltpu.make_async_copy(cols.at[s], cols.at[s], col_recv.at[s]).wait()

    def multiply(d, k):
        row = pl.ds(pl.multiple_of(k * (rows // pieces), 16), rows // pieces)

        def one(n, _):
            sign = 1 - 2 * (n // 4)
            cross = lax.rem(n // 2, 2)
            distance = d - cross
            place = line + sign * distance
            good = jnp.logical_and(place >= 0, place < length)
            good = jnp.logical_and(good, distance >= n // 4)
            good = jnp.logical_and(good, distance >= 0)

            @pl.when(good)
            def _():
                s = index(place, lax.rem(side + cross, 2), lax.rem(n, 2))
                right = cols[s]
                if span != tile:
                    right = jnp.where(offset == aligned, right[:tile], right[span - tile:])
                product = lax.dot_general(
                    full[s, row, :], right, (((1,), (1,)), ((), ())), preferred_element_type=jnp.float32
                )
                for b in range(out_ref.shape[0]):
                    width = min(128, tile - b * 128)
                    out_ref[b, row, :width] += product[:, b * 128:b * 128 + width]

            return 0

        lax.fori_loop(0, 8, one, 0)

    def ready_own(k, _):
        s = index(line, side, 1 - core)
        arrived(s, k)
        to_peers(s, k)
        return 0

    lax.fori_loop(0, chunks, ready_own, 0)
    take_cols(me)
    take_cols(sibling)
    lax.fori_loop(1, length + 1, step, 0)

    def last(k, _):
        multiply(length, k)
        return 0

    lax.fori_loop(0, pieces, last, 0)

    def sent(s, way, first, count):
        ref = full.at[s, pl.ds(first * size, count * size)]
        pltpu.make_async_copy(ref, ref, send.at[way, s]).wait()

    def drain(place, _):
        straight, cross = index(place, side, core), index(place, 1 - side, core)
        sent(straight, 3, 0, chunks)
        sent(cross, 3, 0, chunks)
        pl.when(place == line)(lambda: sent(straight, 2, 0, chunks))
        pl.when(place != line)(lambda: sent(straight, 2, early, chunks - early))

        @pl.when(jnp.logical_and(has_up, place <= line))
        def _():
            sent(straight, 0, 0, chunks)
            sent(cross, 0, 0, early)

        @pl.when(jnp.logical_and(has_down, place >= line))
        def _():
            sent(straight, 1, 0, chunks)
            sent(cross, 1, 0, early)

        return 0

    lax.fori_loop(0, length, drain, 0)

    @pl.when(owns_cols)
    def _():
        for n in range(len(peers)):
            pltpu.make_async_copy(cols, cols, col_send.at[n]).wait()

    for n in range(len(peers)):
        pltpu.make_async_copy(sums.at[i], sums.at[i], sum_send.at[n]).wait()


def flatten(tile, group, gram_ref, flat_ref):
    many = gram_ref.shape[1] // group
    wide = group * tile // 128
    scale = jnp.float32(1.0 / (MEMBERS - 1))
    for s in range(wide):
        parts = []
        at = s * 128
        while at < (s + 1) * 128:
            r, c = at // tile, at % tile
            count = min(tile - c, (s + 1) * 128 - at)
            parts.append((r, c, count, at - s * 128))
            at += count
        lane = lax.broadcasted_iota(jnp.int32, (many, 128), 1)
        value = None
        for r, c, count, to in parts:
            shift = (to - c) % 128
            here = gram_ref[c // 128, pl.ds(r, many, stride=group), :]
            here = pltpu.roll(here, shift, 1) if shift else here
            if c % 128 + count > 128:
                then = gram_ref[c // 128 + 1, pl.ds(r, many, stride=group), :]
                then = pltpu.roll(then, shift, 1) if shift else then
                here = jnp.where(lane < to + 128 - c % 128, here, then)
            value = here if value is None else jnp.where(lane < to, value, here)
        flat_ref[pl.ds(s, many, stride=wide), :] = value * scale


def local(n_row, n_col, snapshots, area_weight):
    rows, depth = snapshots.shape
    tile = rows * n_row // n_col
    units = rows // 16
    chunks = max(n for n in range(1, MAX_CHUNKS + 1) if units % n == 0)
    pieces = max(n for n in range(1, 9) if units % n == 0)
    early = max(1, round(chunks / 6))
    span = tile + tile % 16
    blocks = -(-tile // 128)
    gram = pl.pallas_call(
        functools.partial(gather_gram, n_row, n_col, chunks, early, pieces, tile),
        out_shape=jax.ShapeDtypeStruct((blocks, rows, 128), jnp.float32),
        in_specs=[pl.BlockSpec(memory_space=pltpu.VMEM)] * 2,
        out_specs=pl.BlockSpec(memory_space=pltpu.VMEM),
        scratch_shapes=[
            pltpu.VMEM((n_col, rows, depth), jnp.bfloat16),
            pltpu.VMEM((n_col, span, depth), jnp.bfloat16),
            pltpu.VMEM((n_row, 8, depth), jnp.float32),
            pltpu.SemaphoreType.DMA((n_col, chunks)),
            pltpu.SemaphoreType.DMA((4, n_col)),
            pltpu.SemaphoreType.DMA((n_col,)),
            pltpu.SemaphoreType.DMA((max(n_row - 1, 1),)),
            pltpu.SemaphoreType.DMA((n_row,)),
            pltpu.SemaphoreType.DMA((max(n_row - 1, 1),)),
        ],
        compiler_params=pltpu.CompilerParams(
            collective_id=0, has_side_effects=True, vmem_limit_bytes=60 * 2**20
        ),
        name="gather_gram",
    )(snapshots, area_weight.reshape(1, depth))
    group = 8
    while group * tile % 128:
        group *= 2
    groups = rows // group
    block = max((n for n in range(8, 257, 8) if groups % n == 0), default=groups)
    wide = group * tile // 128
    flat = pl.pallas_call(
        functools.partial(flatten, tile, group),
        grid=(groups // block,),
        out_shape=jax.ShapeDtypeStruct((groups * wide, 128), jnp.float32),
        in_specs=[pl.BlockSpec((blocks, block * group, 128), lambda n: (0, n, 0))],
        out_specs=pl.BlockSpec((block * wide, 128), lambda n: (n, 0)),
        name="flatten",
    )(gram)
    return flat.reshape(1, 1, rows * tile)


def solution(mesh):
    placed = (P("mrow", "pcol"), P("pcol"))
    return jax.shard_map(
        functools.partial(local, mesh.shape["mrow"], mesh.shape["pcol"]),
        mesh=mesh, in_specs=placed, out_specs=P("mrow", "pcol", None), check_vma=False,
    )
```

profile of v0, /device:TPU:27, one launch (start us, length us, event | category | flops | bytes accessed | tf_op | source)
XLA Modules:
  0.0 195.5 jit_solution(17472959858717898632)
XLA Ops:
  0.0 188.2 %gather_gram.1.gram_ref = f32[4,3712,128]{2,1,0:T(8,128)} custom-call(bf16[3712,256]{1,0:T(8,128)(2,1)} %x_ref.1, f32[1,256]{1,0:T(1,128)} %bitcast.2), custom_call_target="tpu_custom_call" | custom-call | tf_op jit(solution)/shard_map/gather_gram/pallas_call | solution.py:321
  188.2 7.4 %flatten.1 = f32[13456,128]{1,0:T(8,128)} custom-call(f32[4,3712,128]{2,1,0:T(8,128)} %gather_gram.1.gram_ref), custom_call_target="tpu_custom_call" | custom-call | tf_op jit(solution)/shard_map/flatten/pallas_call | solution.py:348
where the time goes:
time: 196 us
  Pallas kernels  196 us (100%)
    pallas_call x1, Pallas kernels, local(): pl.pallas_call(functools.partial(gather_gram, n_row, n_col, chunks, early...  188 us
    pallas_call x1, Pallas kernels, local(): pl.pallas_call(functools.partial(flatten, tile, group), grid=(groups // b...  7.35 us

commit v1 on v0

--- a/solution.py
+++ b/solution.py
@@ -12,13 +12,25 @@
 MESH = pl.DeviceIdType.MESH
 
 
+def trigger(n_row, n_col, chunks, size, tile, me):
+    ratio = n_col // n_row
+    root = me // ratio
+    first = me % ratio * tile // 16 * 16
+    last = first + tile + tile % 16 - 1
+    up, down = last // size, chunks - 1 - first // size
+    if isinstance(me, int):
+        return down if 2 * root >= n_row else up
+    return jnp.where(2 * root >= n_row, down, up)
+
+
 def gather_gram(
-    n_row, n_col, chunks, early, pieces, tile, x_ref, weight_ref, out_ref, full, cols, sums, recv, send, col_recv, col_send,
+    n_row, n_col, chunks, quick, tile, x_ref, weight_ref, out_ref, full, cols, sums, recv, send, col_recv, col_send,
     sum_recv, sum_send,
 ):
     rows, depth = x_ref.shape
     length = n_col // 4
     size = rows // chunks
+    half = chunks // 2
     span = cols.shape[1]
     i = lax.axis_index("mrow")
     me = lax.axis_index("pcol")
@@ -29,8 +41,8 @@
     root = me // ratio
     offset = lax.rem(me, ratio) * tile
     aligned = pl.multiple_of(offset // 16 * 16, 16)
-    my_chunk = (aligned + span - 1) // size
-    stride = chunks // pieces
+    my_chunk = trigger(n_row, n_col, chunks, size, tile, me)
+    backward = 2 * i >= n_row
 
     def index(where, which, own):
         return (where * 2 + which) * 2 + own
@@ -40,6 +52,16 @@
     has_up, has_down = line + 1 < length, line >= 1
     peers = [lax.rem(i + step, n_row) for step in range(1, n_row)]
     owns_cols = root == i
+
+    def is_end(place):
+        return jnp.logical_or(place == 0, place == length - 1)
+
+    def first_by_line(place, sign):
+        if not quick:
+            return jnp.int32(chunks)
+        return jnp.where(is_end(place), half, jnp.where(is_end(place + sign), 0, chunks))
+
+    end = is_end(line) if quick else line < 0
 
     barrier = pltpu.get_barrier_semaphore()
 
@@ -60,8 +82,12 @@
     sums[i] = lax.fori_loop(0, chunks, add_up, jnp.zeros((8, depth), jnp.float32))
     pl.semaphore_wait(barrier, 2 + len(peers) + has_up.astype(jnp.int32) + has_down.astype(jnp.int32))
 
+    def rows_of(k):
+        at = jnp.where(backward, chunks - 1 - k, k)
+        return pl.ds(pl.multiple_of(at * size, 16), size)
+
     def part(s, k):
-        return full.at[s, pl.ds(pl.multiple_of(k * size, 16), size)]
+        return full.at[s, rows_of(k)]
 
     def copy(s, k, way, target):
         return pltpu.make_async_remote_copy(
@@ -108,7 +134,7 @@
     root_weight = jnp.sqrt(weight_ref[...])
 
     def center(k):
-        row = pl.ds(pl.multiple_of(k * size, 16), size)
+        row = rows_of(k)
         full[me, row, :] = ((x_ref[row, :].astype(jnp.float32) - mean) * root_weight).astype(jnp.bfloat16)
 
     def own(k, _):
@@ -123,76 +149,84 @@
     center(0)
     lax.fori_loop(0, chunks, own, 0)
 
-    def cross_first(k, _):
-        arrived(across, k)
-        go_up(across, k)
-        go_down(across, k)
-        share(across, k)
-        to_peers(across, k)
-        return 0
-
-    lax.fori_loop(0, early, cross_first, 0)
-
     def valid(sign, distance):
         place = line + sign * distance
         inside = jnp.logical_and(place >= 0, place < length)
         far = distance >= 1 if sign > 0 else distance >= 0
         return jnp.logical_and(inside, far)
 
-    def step(d, _):
-        def from_sibling(k):
-            for sign in (-1, 1):
-                for which, distance in ((side, d), (1 - side, d - 1)):
-                    @pl.when(valid(sign, distance))
-                    def _():
-                        s = index(line + sign * distance, which, 1 - core)
-                        arrived(s, k)
-                        to_peers(s, k)
-
-        def piece(k, _):
-            for sign, forward in ((-1, go_up), (1, go_down)):
-                @pl.when(valid(sign, d))
-                def _():
-                    s = index(line + sign * d, side, core)
-                    arrived(s, k)
-                    forward(s, k)
-                    pl.when(k >= early)(lambda: copy(s, k, 2, across).start())
-                    share(s, k)
-                    to_peers(s, k)
-
-                    @pl.when(k < early)
-                    def _():
-                        t = index(line + sign * d, 1 - side, core)
-                        arrived(t, k)
-                        forward(t, k)
-                        share(t, k)
-                        to_peers(t, k)
-
-            for sign in (-1, 1):
-                @pl.when(jnp.logical_and(valid(sign, d - 1), k >= early))
-                def _():
-                    s = index(line + sign * (d - 1), 1 - side, core)
-                    arrived(s, k)
-                    share(s, k)
-                    to_peers(s, k)
-
-            pl.when(k >= 1)(lambda: from_sibling(k - 1))
-
-            @pl.when(jnp.logical_and(lax.rem(k, stride) == stride - 1, k // stride < pieces))
+    def is_late(distance, k):
+        return jnp.logical_and(end, jnp.logical_and(distance == 1, k >= half))
+
+    near = jnp.where(line == 0, 1, line - 1)
+
+    def from_sibling(t):
+        d, k = t // chunks + 1, lax.rem(t, chunks)
+
+        def take(s):
+            arrived(s, k)
+            to_peers(s, k)
+
+        for sign in (-1, 1):
+            pl.when(valid(sign, d))(lambda: take(index(line + sign * d, side, 1 - core)))
+            pl.when(jnp.logical_and(valid(sign, d - 1), jnp.logical_not(is_late(d - 1, k))))(
+                lambda: take(index(line + sign * (d - 1), 1 - side, 1 - core))
+            )
+        pl.when(jnp.logical_and(d == length, is_late(1, k)))(lambda: take(index(near, 1 - side, 1 - core)))
+
+    def repeat(way, target, start):
+        def one(k, _):
+            copy(across, k, way, target).start()
+            return 0
+
+        lax.fori_loop(start, chunks, one, 0)
+
+    def slot(t, _):
+        d, k = t // chunks + 1, lax.rem(t, chunks)
+        for sign, forward in ((-1, go_up), (1, go_down)):
+            @pl.when(valid(sign, d))
             def _():
-                multiply(d - 1, k // stride)
-
-            return 0
-
-        lax.fori_loop(0, chunks, piece, 0)
-        from_sibling(chunks - 1)
+                s = index(line + sign * d, side, core)
+                arrived(s, k)
+                forward(s, k)
+                by_line = jnp.logical_and(d == 1, k >= first_by_line(line, sign))
+                pl.when(jnp.logical_not(by_line))(lambda: copy(s, k, 2, across).start())
+                share(s, k)
+                to_peers(s, k)
+
+        def take(s):
+            arrived(s, k)
+            share(s, k)
+            to_peers(s, k)
+
         for sign in (-1, 1):
-            for which, distance in ((side, d), (1 - side, d - 1)):
-                for other in (core, 1 - core):
-                    pl.when(valid(sign, distance))(
-                        lambda: take_cols(index(line + sign * distance, which, other))
-                    )
+            pl.when(jnp.logical_and(valid(sign, d - 1), jnp.logical_not(is_late(d - 1, k))))(
+                lambda: take(index(line + sign * (d - 1), 1 - side, core))
+            )
+        pl.when(jnp.logical_and(d == length, is_late(1, k)))(lambda: take(index(near, 1 - side, core)))
+        pl.when(t >= 1)(lambda: from_sibling(t - 1))
+
+        @pl.when(jnp.logical_and(k == chunks - 1, jnp.logical_and(has_up, d == jnp.maximum(line, 1))))
+        def _():
+            repeat(0, up, first_by_line(line + 1, -1))
+
+        @pl.when(jnp.logical_and(k == chunks - 1, jnp.logical_and(has_down, d == jnp.maximum(length - 1 - line, 1))))
+        def _():
+            repeat(1, down, first_by_line(line - 1, 1))
+
+        lax.fori_loop(done(t - 1), done(t), lambda v, _: work(v), 0)
+
+        @pl.when(jnp.logical_and(d == length, jnp.logical_and(k > half, end)))
+        def _():
+            late(k - 1)
+
         return 0
+
+    lag = chunks + 1
+    hurry = chunks * length - max(1, chunks // 4) if quick else chunks * length
+
+    def done(t):
+        return jnp.where(t >= hurry, t + chunks, jnp.maximum(t + chunks - lag, 0))
 
     def take_cols(s):
         @pl.when(owns_cols)
@@ -203,8 +237,20 @@
         def _():
             pltpu.make_async_copy(cols.at[s], cols.at[s], col_recv.at[s]).wait()
 
-    def multiply(d, k):
-        row = pl.ds(pl.multiple_of(k * (rows // pieces), 16), rows // pieces)
+    def add_product(s, k):
+        row = rows_of(k)
+        right = cols[s]
+        if span != tile:
+            right = jnp.where(offset == aligned, right[:tile], right[span - tile:])
+        product = lax.dot_general(
+            full[s, row, :], right, (((1,), (1,)), ((), ())), preferred_element_type=jnp.float32
+        )
+        for b in range(out_ref.shape[0]):
+            width = min(128, tile - b * 128)
+            out_ref[b, row, :width] += product[:, b * 128:b * 128 + width]
+
+    def work(v):
+        d, k = v // chunks, lax.rem(v, chunks)
 
         def one(n, _):
             sign = 1 - 2 * (n // 4)
@@ -214,23 +260,25 @@
             good = jnp.logical_and(place >= 0, place < length)
             good = jnp.logical_and(good, distance >= n // 4)
             good = jnp.logical_and(good, distance >= 0)
+            good = jnp.logical_and(good, jnp.logical_not(jnp.logical_and(cross == 1, is_late(distance, k))))
 
             @pl.when(good)
             def _():
                 s = index(place, lax.rem(side + cross, 2), lax.rem(n, 2))
-                right = cols[s]
-                if span != tile:
-                    right = jnp.where(offset == aligned, right[:tile], right[span - tile:])
-                product = lax.dot_general(
-                    full[s, row, :], right, (((1,), (1,)), ((), ())), preferred_element_type=jnp.float32
-                )
-                for b in range(out_ref.shape[0]):
-                    width = min(128, tile - b * 128)
-                    out_ref[b, row, :width] += product[:, b * 128:b * 128 + width]
+                pl.when(k == 0)(lambda: take_cols(s))
+                add_product(s, k)
 
             return 0
 
         lax.fori_loop(0, 8, one, 0)
+        return 0
+
+    def late(k):
+        def one(n, _):
+            add_product(index(near, 1 - side, n), k)
+            return 0
+
+        lax.fori_loop(0, 2, one, 0)
 
     def ready_own(k, _):
         s = index(line, side, 1 - core)
@@ -239,36 +287,35 @@
         return 0
 
     lax.fori_loop(0, chunks, ready_own, 0)
-    take_cols(me)
-    take_cols(sibling)
-    lax.fori_loop(1, length + 1, step, 0)
-
-    def last(k, _):
-        multiply(length, k)
-        return 0
-
-    lax.fori_loop(0, pieces, last, 0)
-
-    def sent(s, way, first, count):
-        ref = full.at[s, pl.ds(first * size, count * size)]
+    last = chunks * length - 1
+    lax.fori_loop(0, last + 1, slot, 0)
+    from_sibling(last)
+    lax.fori_loop(done(last), chunks * (length + 1), lambda v, _: work(v), 0)
+    pl.when(end)(lambda: late(chunks - 1))
+
+    def sent(s, way, count):
+        ref = full.at[s, pl.ds(0, count * size)]
         pltpu.make_async_copy(ref, ref, send.at[way, s]).wait()
+
+    def some_sent(s, way, count):
+        pl.when(count == chunks)(lambda: sent(s, way, chunks))
+        if quick:
+            pl.when(count == half)(lambda: sent(s, way, half))
 
     def drain(place, _):
         straight, cross = index(place, side, core), index(place, 1 - side, core)
-        sent(straight, 3, 0, chunks)
-        sent(cross, 3, 0, chunks)
-        pl.when(place == line)(lambda: sent(straight, 2, 0, chunks))
-        pl.when(place != line)(lambda: sent(straight, 2, early, chunks - early))
-
-        @pl.when(jnp.logical_and(has_up, place <= line))
-        def _():
-            sent(straight, 0, 0, chunks)
-            sent(cross, 0, 0, early)
-
-        @pl.when(jnp.logical_and(has_down, place >= line))
-        def _():
-            sent(straight, 1, 0, chunks)
-            sent(cross, 1, 0, early)
+        sent(straight, 3, chunks)
+        sent(cross, 3, chunks)
+        beside = jnp.logical_or(place == line + 1, place == line - 1)
+        sign = place - line
+        some_sent(straight, 2, jnp.where(beside, first_by_line(line, sign), chunks))
+        pl.when(jnp.logical_and(has_up, place <= line))(lambda: sent(straight, 0, chunks))
+        pl.when(jnp.logical_and(has_down, place >= line))(lambda: sent(straight, 1, chunks))
+
+        @pl.when(place == line)
+        def _():
+            pl.when(has_up)(lambda: some_sent(cross, 0, chunks - first_by_line(line + 1, -1)))
+            pl.when(has_down)(lambda: some_sent(cross, 1, chunks - first_by_line(line - 1, 1)))
 
         return 0
 
@@ -314,12 +361,14 @@
     tile = rows * n_row // n_col
     units = rows // 16
     chunks = max(n for n in range(1, MAX_CHUNKS + 1) if units % n == 0)
-    pieces = max(n for n in range(1, 9) if units % n == 0)
-    early = max(1, round(chunks / 6))
+    size = rows // chunks
+    length = n_col // 4
+    ends = [*range(4), *range(n_col - 4, n_col)]
+    quick = length > 2 and all(trigger(n_row, n_col, chunks, size, tile, me) < chunks // 2 for me in ends)
     span = tile + tile % 16
     blocks = -(-tile // 128)
     gram = pl.pallas_call(
-        functools.partial(gather_gram, n_row, n_col, chunks, early, pieces, tile),
+        functools.partial(gather_gram, n_row, n_col, chunks, quick, tile),
         out_shape=jax.ShapeDtypeStruct((blocks, rows, 128), jnp.float32),
         in_specs=[pl.BlockSpec(memory_space=pltpu.VMEM)] * 2,
         out_specs=pl.BlockSpec(memory_space=pltpu.VMEM),

time: 196 us -> 176 us (0.90)
  the two profiles are of different devices: /device:TPU:27 before, /device:TPU:0 now
where the time goes in v1:
time: 176 us
  Pallas kernels  176 us (100%)
    pallas_call x1, Pallas kernels, local(): pl.pallas_call(functools.partial(gather_gram, n_row, n_col, chunks, quick...  169 us
    pallas_call x1, Pallas kernels, local(): pl.pallas_call(functools.partial(flatten, tile, group), grid=(groups // b...  7.35 us

profile of v1, /device:TPU:0, one launch (start us, length us, event | category | flops | bytes accessed | tf_op | source)
XLA Modules:
  0.0 176.1 jit_solution(6930291627241512287)
XLA Ops:
  0.0 168.7 %gather_gram.1.gram_ref = f32[4,3712,128]{2,1,0:T(8,128)} custom-call(bf16[3712,256]{1,0:T(8,128)(2,1)} %x_ref.1, f32[1,256]{1,0:T(1,128)} %bitcast.2), custom_call_target="tpu_custom_call" | custom-call | tf_op jit(solution)/shard_map/gather_gram/pallas_call | solution.py:370
  168.7 7.4 %flatten.1 = f32[13456,128]{1,0:T(8,128)} custom-call(f32[4,3712,128]{2,1,0:T(8,128)} %gather_gram.1.gram_ref), custom_call_target="tpu_custom_call" | custom-call | tf_op jit(solution)/shard_map/flatten/pallas_call | solution.py:397

commit v2 on v1

--- a/solution.py
+++ b/solution.py
@@ -24,8 +24,8 @@
 
 
 def gather_gram(
-    n_row, n_col, chunks, quick, tile, x_ref, weight_ref, out_ref, full, cols, sums, recv, send, col_recv, col_send,
-    sum_recv, sum_send,
+    n_row, n_col, chunks, quick, tile, x_ref, weight_ref, result_ref, out_ref, full, cols, sums, recv, send, col_recv, col_send,
+    sum_recv, sum_send, out_sem,
 ):
     rows, depth = x_ref.shape
     length = n_col // 4
@@ -155,24 +155,29 @@
         far = distance >= 1 if sign > 0 else distance >= 0
         return jnp.logical_and(inside, far)
 
-    def is_late(distance, k):
-        return jnp.logical_and(end, jnp.logical_and(distance == 1, k >= half))
-
     near = jnp.where(line == 0, 1, line - 1)
+    final = chunks * (length - 1)
+    slots = final + (half if quick else chunks)
+
+    def cross_at(t):
+        w = t + jnp.where(jnp.logical_and(end, t >= chunks + half), half, 0)
+        return w // chunks, lax.rem(w, chunks)
+
+    def late_at(t):
+        return jnp.logical_and(end, t >= final), t - final + half
 
     def from_sibling(t):
-        d, k = t // chunks + 1, lax.rem(t, chunks)
-
-        def take(s):
+        def take(s, k):
             arrived(s, k)
             to_peers(s, k)
 
+        d, k = t // chunks + 1, lax.rem(t, chunks)
+        e, m = cross_at(t)
         for sign in (-1, 1):
-            pl.when(valid(sign, d))(lambda: take(index(line + sign * d, side, 1 - core)))
-            pl.when(jnp.logical_and(valid(sign, d - 1), jnp.logical_not(is_late(d - 1, k))))(
-                lambda: take(index(line + sign * (d - 1), 1 - side, 1 - core))
-            )
-        pl.when(jnp.logical_and(d == length, is_late(1, k)))(lambda: take(index(near, 1 - side, 1 - core)))
+            pl.when(valid(sign, d))(lambda: take(index(line + sign * d, side, 1 - core), k))
+            pl.when(valid(sign, e))(lambda: take(index(line + sign * e, 1 - side, 1 - core), m))
+        is_late, m = late_at(t)
+        pl.when(is_late)(lambda: take(index(near, 1 - side, 1 - core), m))
 
     def repeat(way, target, start):
         def one(k, _):
@@ -194,16 +199,16 @@
                 share(s, k)
                 to_peers(s, k)
 
-        def take(s):
-            arrived(s, k)
-            share(s, k)
-            to_peers(s, k)
-
+        def take(s, m):
+            arrived(s, m)
+            share(s, m)
+            to_peers(s, m)
+
+        e, m = cross_at(t)
         for sign in (-1, 1):
-            pl.when(jnp.logical_and(valid(sign, d - 1), jnp.logical_not(is_late(d - 1, k))))(
-                lambda: take(index(line + sign * (d - 1), 1 - side, core))
-            )
-        pl.when(jnp.logical_and(d == length, is_late(1, k)))(lambda: take(index(near, 1 - side, core)))
+            pl.when(valid(sign, e))(lambda: take(index(line + sign * e, 1 - side, core), m))
+        is_late, n = late_at(t)
+        pl.when(is_late)(lambda: take(index(near, 1 - side, core), n))
         pl.when(t >= 1)(lambda: from_sibling(t - 1))
 
         @pl.when(jnp.logical_and(k == chunks - 1, jnp.logical_and(has_up, d == jnp.maximum(line, 1))))
@@ -216,17 +221,15 @@
 
         lax.fori_loop(done(t - 1), done(t), lambda v, _: work(v), 0)
 
-        @pl.when(jnp.logical_and(d == length, jnp.logical_and(k > half, end)))
-        def _():
-            late(k - 1)
-
-        return 0
-
-    lag = chunks + 1
-    hurry = chunks * length - max(1, chunks // 4) if quick else chunks * length
+        was_late, m = late_at(t - 1)
+        pl.when(was_late)(lambda: late(m))
+        return 0
 
     def done(t):
-        return jnp.where(t >= hurry, t + chunks, jnp.maximum(t + chunks - lag, 0))
+        lag = jnp.full_like(t, chunks + 1)
+        if quick:
+            lag = jnp.where(t >= final - half * end.astype(jnp.int32), jnp.maximum(1, chunks - half - (t - final)), lag)
+        return jnp.maximum(t + chunks + 1 - lag, 0)
 
     def take_cols(s):
         @pl.when(owns_cols)
@@ -250,17 +253,17 @@
             out_ref[b, row, :width] += product[:, b * 128:b * 128 + width]
 
     def work(v):
-        d, k = v // chunks, lax.rem(v, chunks)
+        e, m = cross_at(v - chunks)
 
         def one(n, _):
             sign = 1 - 2 * (n // 4)
             cross = lax.rem(n // 2, 2)
-            distance = d - cross
+            distance = jnp.where(cross == 1, e, v // chunks)
+            k = jnp.where(cross == 1, m, lax.rem(v, chunks))
             place = line + sign * distance
             good = jnp.logical_and(place >= 0, place < length)
             good = jnp.logical_and(good, distance >= n // 4)
-            good = jnp.logical_and(good, distance >= 0)
-            good = jnp.logical_and(good, jnp.logical_not(jnp.logical_and(cross == 1, is_late(distance, k))))
+            good = jnp.logical_and(good, jnp.logical_or(cross == 0, v >= chunks))
 
             @pl.when(good)
             def _():
@@ -287,11 +290,24 @@
         return 0
 
     lax.fori_loop(0, chunks, ready_own, 0)
-    last = chunks * length - 1
-    lax.fori_loop(0, last + 1, slot, 0)
+    lax.fori_loop(0, slots, slot, 0)
+
+    def out_copy(k):
+        row = rows_of(k)
+        return pltpu.make_async_copy(out_ref.at[:, row, :], result_ref.at[:, row, :], out_sem)
+
+    early = chunks - 1 if quick else 0
+
+    def leave(k, _):
+        out_copy(k).start()
+        return 0
+
+    lax.fori_loop(0, early, leave, 0)
+    last = jnp.int32(slots - 1)
     from_sibling(last)
-    lax.fori_loop(done(last), chunks * (length + 1), lambda v, _: work(v), 0)
+    lax.fori_loop(done(last), slots + chunks, lambda v, _: work(v), 0)
     pl.when(end)(lambda: late(chunks - 1))
+    lax.fori_loop(early, chunks, leave, 0)
 
     def sent(s, way, count):
         ref = full.at[s, pl.ds(0, count * size)]
@@ -328,6 +344,7 @@
 
     for n in range(len(peers)):
         pltpu.make_async_copy(sums.at[i], sums.at[i], sum_send.at[n]).wait()
+    pltpu.make_async_copy(out_ref, result_ref, out_sem).wait()
 
 
 def flatten(tile, group, gram_ref, flat_ref):
@@ -371,8 +388,9 @@
         functools.partial(gather_gram, n_row, n_col, chunks, quick, tile),
         out_shape=jax.ShapeDtypeStruct((blocks, rows, 128), jnp.float32),
         in_specs=[pl.BlockSpec(memory_space=pltpu.VMEM)] * 2,
-        out_specs=pl.BlockSpec(memory_space=pltpu.VMEM),
+        out_specs=pl.BlockSpec(memory_space=pl.ANY),
         scratch_shapes=[
+            pltpu.VMEM((blocks, rows, 128), jnp.float32),
             pltpu.VMEM((n_col, rows, depth), jnp.bfloat16),
             pltpu.VMEM((n_col, span, depth), jnp.bfloat16),
             pltpu.VMEM((n_row, 8, depth), jnp.float32),
@@ -382,6 +400,7 @@
             pltpu.SemaphoreType.DMA((max(n_row - 1, 1),)),
             pltpu.SemaphoreType.DMA((n_row,)),
             pltpu.SemaphoreType.DMA((max(n_row - 1, 1),)),
+            pltpu.SemaphoreType.DMA,
         ],
         compiler_params=pltpu.CompilerParams(
             collective_id=0, has_side_effects=True, vmem_limit_bytes=60 * 2**20
@@ -396,7 +415,7 @@
     wide = group * tile // 128
     flat = pl.pallas_call(
         functools.partial(flatten, tile, group),
-        grid=(groups // block,),
+        grid=(pl.cdiv(groups, block),),
         out_shape=jax.ShapeDtypeStruct((groups * wide, 128), jnp.float32),
         in_specs=[pl.BlockSpec((blocks, block * group, 128), lambda n: (0, n, 0))],
         out_specs=pl.BlockSpec((block * wide, 128), lambda n: (n, 0)),

time: 176 us -> 167 us (0.949)
  Pallas kernels: 176 us -> 166 us
    pallas_call x1, Pallas kernels: 169 us -> 159 us  [local(): pl.pallas_call(functools.partial(gather_gram, n_row, n_col, chunks, quick...]
where the time goes in v2:
time: 167 us; the launch traced here: 166 us
  Pallas kernels  166 us (99%)
    pallas_call x1, Pallas kernels, local(): pl.pallas_call(functools.partial(gather_gram, n_row, n_col, chunks, quick...  159 us
    pallas_call x1, Pallas kernels, local(): pl.pallas_call(functools.partial(flatten, tile, group), grid=(pl.cdiv(gro...  7.35 us

profile of v2, /device:TPU:0, one launch (start us, length us, event | category | flops | bytes accessed | tf_op | source)
XLA Modules:
  0.0 166.4 jit_solution(13196669268262381984)
XLA Ops:
  0.0 159.0 %gather_gram.1.gram_ref = f32[4,3712,128]{2,1,0:T(8,128)} custom-call(bf16[3712,256]{1,0:T(8,128)(2,1)} %x_ref.1, f32[1,256]{1,0:T(1,128)} %bitcast.2), custom_call_target="tpu_custom_call" | custom-call | tf_op jit(solution)/shard_map/gather_gram/pallas_call | solution.py:387
  159.1 7.4 %flatten.1 = f32[13456,128]{1,0:T(8,128)} custom-call(f32[4,3712,128]{2,1,0:T(8,128)} %gather_gram.1.gram_ref), custom_call_target="tpu_custom_call" | custom-call | tf_op jit(solution)/shard_map/flatten/pallas_call | solution.py:416

commit v3 on v2

--- a/solution.py
+++ b/solution.py
@@ -9,6 +9,7 @@
 
 MEMBERS = 7424
 MAX_CHUNKS = 8
+PIECES = 6
 MESH = pl.DeviceIdType.MESH
 
 
@@ -24,8 +25,8 @@
 
 
 def gather_gram(
-    n_row, n_col, chunks, quick, tile, x_ref, weight_ref, result_ref, out_ref, full, cols, sums, recv, send, col_recv, col_send,
-    sum_recv, sum_send, out_sem,
+    n_row, n_col, chunks, quick, tile, x_ref, weight_ref, out_ref, full, cols, sums, recv, send, col_recv, col_send,
+    sum_recv, sum_send,
 ):
     rows, depth = x_ref.shape
     length = n_col // 4
@@ -292,22 +293,10 @@
     lax.fori_loop(0, chunks, ready_own, 0)
     lax.fori_loop(0, slots, slot, 0)
 
-    def out_copy(k):
-        row = rows_of(k)
-        return pltpu.make_async_copy(out_ref.at[:, row, :], result_ref.at[:, row, :], out_sem)
-
-    early = chunks - 1 if quick else 0
-
-    def leave(k, _):
-        out_copy(k).start()
-        return 0
-
-    lax.fori_loop(0, early, leave, 0)
     last = jnp.int32(slots - 1)
     from_sibling(last)
     lax.fori_loop(done(last), slots + chunks, lambda v, _: work(v), 0)
     pl.when(end)(lambda: late(chunks - 1))
-    lax.fori_loop(early, chunks, leave, 0)
 
     def sent(s, way, count):
         ref = full.at[s, pl.ds(0, count * size)]
@@ -344,33 +333,35 @@
 
     for n in range(len(peers)):
         pltpu.make_async_copy(sums.at[i], sums.at[i], sum_send.at[n]).wait()
-    pltpu.make_async_copy(out_ref, result_ref, out_sem).wait()
-
-
-def flatten(tile, group, gram_ref, flat_ref):
-    many = gram_ref.shape[1] // group
+
+
+def flatten(tile, group, block, gram_ref, flat_ref, buffer, sem):
+    groups = gram_ref.shape[1] // group
     wide = group * tile // 128
     scale = jnp.float32(1.0 / (MEMBERS - 1))
-    for s in range(wide):
-        parts = []
-        at = s * 128
-        while at < (s + 1) * 128:
-            r, c = at // tile, at % tile
-            count = min(tile - c, (s + 1) * 128 - at)
-            parts.append((r, c, count, at - s * 128))
-            at += count
+    for start in range(0, groups, block):
+        many = min(block, groups - start)
         lane = lax.broadcasted_iota(jnp.int32, (many, 128), 1)
-        value = None
-        for r, c, count, to in parts:
-            shift = (to - c) % 128
-            here = gram_ref[c // 128, pl.ds(r, many, stride=group), :]
-            here = pltpu.roll(here, shift, 1) if shift else here
-            if c % 128 + count > 128:
-                then = gram_ref[c // 128 + 1, pl.ds(r, many, stride=group), :]
-                then = pltpu.roll(then, shift, 1) if shift else then
-                here = jnp.where(lane < to + 128 - c % 128, here, then)
-            value = here if value is None else jnp.where(lane < to, value, here)
-        flat_ref[pl.ds(s, many, stride=wide), :] = value * scale
+        for s in range(wide):
+            value = None
+            at = s * 128
+            while at < (s + 1) * 128:
+                r, c, to = at // tile, at % tile, at - s * 128
+                count = min(tile - c, (s + 1) * 128 - at)
+                shift = (to - c) % 128
+                row = pl.ds(start * group + r, many, stride=group)
+                here = gram_ref[c // 128, row, :]
+                here = pltpu.roll(here, shift, 1) if shift else here
+                if c % 128 + count > 128:
+                    then = gram_ref[c // 128 + 1, row, :]
+                    then = pltpu.roll(then, shift, 1) if shift else then
+                    here = jnp.where(lane < to + 128 - c % 128, here, then)
+                value = here if value is None else jnp.where(lane < to, value, here)
+                at += count
+            buffer[pl.ds(start * wide + s, many, stride=wide), :] = value * scale
+        piece = pl.ds(start * wide, many * wide)
+        pltpu.make_async_copy(buffer.at[piece], flat_ref.at[piece], sem).start()
+    pltpu.make_async_copy(buffer, flat_ref, sem).wait()
 
 
 def local(n_row, n_col, snapshots, area_weight):
@@ -388,9 +379,8 @@
         functools.partial(gather_gram, n_row, n_col, chunks, quick, tile),
         out_shape=jax.ShapeDtypeStruct((blocks, rows, 128), jnp.float32),
         in_specs=[pl.BlockSpec(memory_space=pltpu.VMEM)] * 2,
-        out_specs=pl.BlockSpec(memory_space=pl.ANY),
+        out_specs=pl.BlockSpec(memory_space=pltpu.VMEM),
         scratch_shapes=[
-            pltpu.VMEM((blocks, rows, 128), jnp.float32),
             pltpu.VMEM((n_col, rows, depth), jnp.bfloat16),
             pltpu.VMEM((n_col, span, depth), jnp.bfloat16),
             pltpu.VMEM((n_row, 8, depth), jnp.float32),
@@ -400,10 +390,9 @@
             pltpu.SemaphoreType.DMA((max(n_row - 1, 1),)),
             pltpu.SemaphoreType.DMA((n_row,)),
             pltpu.SemaphoreType.DMA((max(n_row - 1, 1),)),
-            pltpu.SemaphoreType.DMA,
         ],
         compiler_params=pltpu.CompilerParams(
-            collective_id=0, has_side_effects=True, vmem_limit_bytes=60 * 2**20
+            collective_id=0, has_side_effects=True, vmem_limit_bytes=44 * 2**20
         ),
         name="gather_gram",
     )(snapshots, area_weight.reshape(1, depth))
@@ -411,14 +400,15 @@
     while group * tile % 128:
         group *= 2
     groups = rows // group
-    block = max((n for n in range(8, 257, 8) if groups % n == 0), default=groups)
-    wide = group * tile // 128
+    block = (groups // PIECES + 7) // 8 * 8
+    flat_shape = (groups * group * tile // 128, 128)
     flat = pl.pallas_call(
-        functools.partial(flatten, tile, group),
-        grid=(pl.cdiv(groups, block),),
-        out_shape=jax.ShapeDtypeStruct((groups * wide, 128), jnp.float32),
-        in_specs=[pl.BlockSpec((blocks, block * group, 128), lambda n: (0, n, 0))],
-        out_specs=pl.BlockSpec((block * wide, 128), lambda n: (n, 0)),
+        functools.partial(flatten, tile, group, block),
+        out_shape=jax.ShapeDtypeStruct(flat_shape, jnp.float32),
+        in_specs=[pl.BlockSpec(memory_space=pltpu.VMEM)],
+        out_specs=pl.BlockSpec(memory_space=pl.ANY),
+        scratch_shapes=[pltpu.VMEM(flat_shape, jnp.float32), pltpu.SemaphoreType.DMA],
+        compiler_params=pltpu.CompilerParams(vmem_limit_bytes=24 * 2**20),
         name="flatten",
     )(gram)
     return flat.reshape(1, 1, rows * tile)

time: 167 us -> 163 us (0.976)
  Pallas kernels: 166 us -> 161 us
  local copies, waits for them, and re-layouts: 0 us -> 2.2 us
    pallas_call x1, Pallas kernels: 7.35 us -> 4.31 us  [local(): pl.pallas_call(functools.partial(flatten, tile, group, block), out_shape=...]
    pallas_call x1, Pallas kernels: 159 us -> 156 us  [local(): pl.pallas_call(functools.partial(gather_gram, n_row, n_col, chunks, quick...]
    unnamed x0 -> x4, local copies, waits for them, and re-layouts: none -> 2.2 us
where the time goes in v3:
time: 163 us
  Pallas kernels  161 us (99%)
  local copies, waits for them, and re-layouts  2.2 us (1%)
    pallas_call x1, Pallas kernels, local(): pl.pallas_call(functools.partial(gather_gram, n_row, n_col, chunks, quick...  156 us
    pallas_call x1, Pallas kernels, local(): pl.pallas_call(functools.partial(flatten, tile, group, block), out_shape=...  4.31 us

profile of v3, /device:TPU:0, one launch (start us, length us, event | category | flops | bytes accessed | tf_op | source)
XLA Modules:
  0.0 162.8 jit_solution(8566514724414207545)
XLA Ops:
  0.0 0.0 copy-start
  0.0 1.5 copy-done
  1.5 0.0 copy-start.1
  1.5 0.7 copy-done.1
  2.2 156.3 %gather_gram.1.gram_ref = f32[4,3712,128]{2,1,0:T(8,128)S(1)} custom-call(bf16[3712,256]{1,0:T(8,128)(2,1)S(1)} %copy-done, f32[1,256]{1,0:T(1,128)S(1)} %bitcast.2), custom_call_target="tpu_custom_call" | custom-call | tf_op jit(solution)/shard_map/gather_gram/pallas_call | solution.py:378
  158.5 4.3 %flatten.1 = f32[13456,128]{1,0:T(8,128)} custom-call(f32[4,3712,128]{2,1,0:T(8,128)S(1)} %gather_gram.1.gram_ref), custom_call_target="tpu_custom_call" | custom-call | tf_op jit(solution)/shard_map/flatten/pallas_call | solution.py:405
Async XLA Ops:
  0.0 1.5 copy-start
  1.5 0.7 copy-start.1

commit v4 on v3

--- a/solution.py
+++ b/solution.py
@@ -83,12 +83,19 @@
     sums[i] = lax.fori_loop(0, chunks, add_up, jnp.zeros((8, depth), jnp.float32))
     pl.semaphore_wait(barrier, 2 + len(peers) + has_up.astype(jnp.int32) + has_down.astype(jnp.int32))
 
-    def rows_of(k):
-        at = jnp.where(backward, chunks - 1 - k, k)
+    def swapped(s, k):
+        if not quick:
+            return k
+        swap = jnp.logical_and((lax.rem(s // 2, 2) == 0) != backward, k < half)
+        return jnp.where(swap, lax.rem(k + half // 2, half), k)
+
+    def rows_of(s, k):
+        at = swapped(s, k)
+        at = jnp.where(backward, chunks - 1 - at, at)
         return pl.ds(pl.multiple_of(at * size, 16), size)
 
     def part(s, k):
-        return full.at[s, rows_of(k)]
+        return full.at[s, rows_of(s, k)]
 
     def copy(s, k, way, target):
         return pltpu.make_async_remote_copy(
@@ -109,7 +116,7 @@
         copy(s, k, 3, sibling).start()
 
     def to_peers(s, k):
-        @pl.when(jnp.logical_and(owns_cols, k == my_chunk))
+        @pl.when(jnp.logical_and(owns_cols, swapped(s, k) == my_chunk))
         def _():
             for n in range(len(peers)):
                 col_copy(s, n).start()
@@ -135,7 +142,7 @@
     root_weight = jnp.sqrt(weight_ref[...])
 
     def center(k):
-        row = rows_of(k)
+        row = rows_of(me, k)
         full[me, row, :] = ((x_ref[row, :].astype(jnp.float32) - mean) * root_weight).astype(jnp.bfloat16)
 
     def own(k, _):
@@ -179,6 +186,18 @@
             pl.when(valid(sign, e))(lambda: take(index(line + sign * e, 1 - side, 1 - core), m))
         is_late, m = late_at(t)
         pl.when(is_late)(lambda: take(index(near, 1 - side, 1 - core), m))
+
+    def from_across(t):
+        def take(s, k):
+            arrived(s, k)
+            share(s, k)
+            to_peers(s, k)
+
+        e, m = cross_at(t)
+        for sign in (-1, 1):
+            pl.when(valid(sign, e))(lambda: take(index(line + sign * e, 1 - side, core), m))
+        is_late, n = late_at(t)
+        pl.when(is_late)(lambda: take(index(near, 1 - side, core), n))
 
     def repeat(way, target, start):
         def one(k, _):
@@ -200,16 +219,7 @@
                 share(s, k)
                 to_peers(s, k)
 
-        def take(s, m):
-            arrived(s, m)
-            share(s, m)
-            to_peers(s, m)
-
-        e, m = cross_at(t)
-        for sign in (-1, 1):
-            pl.when(valid(sign, e))(lambda: take(index(line + sign * e, 1 - side, core), m))
-        is_late, n = late_at(t)
-        pl.when(is_late)(lambda: take(index(near, 1 - side, core), n))
+        from_across(t)
         pl.when(t >= 1)(lambda: from_sibling(t - 1))
 
         @pl.when(jnp.logical_and(k == chunks - 1, jnp.logical_and(has_up, d == jnp.maximum(line, 1))))
@@ -222,15 +232,27 @@
 
         lax.fori_loop(done(t - 1), done(t), lambda v, _: work(v), 0)
 
-        was_late, m = late_at(t - 1)
-        pl.when(was_late)(lambda: late(m))
         return 0
 
     def done(t):
         lag = jnp.full_like(t, chunks + 1)
         if quick:
-            lag = jnp.where(t >= final - half * end.astype(jnp.int32), jnp.maximum(1, chunks - half - (t - final)), lag)
+            lag = jnp.where(jnp.logical_and(end, t >= final - half), chunks - half - (t - final), lag)
         return jnp.maximum(t + chunks + 1 - lag, 0)
+
+    def end_slot(t, behind):
+        from_sibling(t - 1)
+        now = chunks + final - half + 1 + 2 * (t - final)
+        lax.fori_loop(behind, now, lambda v, _: work(v), 0)
+        was_late, m = late_at(t - 1)
+
+        @pl.when(was_late)
+        def _():
+            late(m, 0)
+            late(m, 1)
+
+        from_across(t)
+        return now
 
     def take_cols(s):
         @pl.when(owns_cols)
@@ -242,7 +264,7 @@
             pltpu.make_async_copy(cols.at[s], cols.at[s], col_recv.at[s]).wait()
 
     def add_product(s, k):
-        row = rows_of(k)
+        row = rows_of(s, k)
         right = cols[s]
         if span != tile:
             right = jnp.where(offset == aligned, right[:tile], right[span - tile:])
@@ -253,7 +275,7 @@
             width = min(128, tile - b * 128)
             out_ref[b, row, :width] += product[:, b * 128:b * 128 + width]
 
-    def work(v):
+    def work(v, lane=None):
         e, m = cross_at(v - chunks)
 
         def one(n, _):
@@ -265,6 +287,8 @@
             good = jnp.logical_and(place >= 0, place < length)
             good = jnp.logical_and(good, distance >= n // 4)
             good = jnp.logical_and(good, jnp.logical_or(cross == 0, v >= chunks))
+            if lane is not None:
+                good = jnp.logical_and(good, lax.rem(n, 2) == lane)
 
             @pl.when(good)
             def _():
@@ -277,12 +301,8 @@
         lax.fori_loop(0, 8, one, 0)
         return 0
 
-    def late(k):
-        def one(n, _):
-            add_product(index(near, 1 - side, n), k)
-            return 0
-
-        lax.fori_loop(0, 2, one, 0)
+    def late(k, lane):
+        add_product(index(near, 1 - side, lane), k)
 
     def ready_own(k, _):
         s = index(line, side, 1 - core)
@@ -291,12 +311,22 @@
         return 0
 
     lax.fori_loop(0, chunks, ready_own, 0)
-    lax.fori_loop(0, slots, slot, 0)
-
     last = jnp.int32(slots - 1)
-    from_sibling(last)
-    lax.fori_loop(done(last), slots + chunks, lambda v, _: work(v), 0)
-    pl.when(end)(lambda: late(chunks - 1))
+    if quick:
+        lax.fori_loop(0, final, slot, 0)
+        lax.fori_loop(final, slots, end_slot, done(jnp.int32(final - 1)))
+
+        def finish(lane):
+            work(last + chunks, lane)
+            pl.when(end)(lambda: late(chunks - 1, lane))
+
+        finish(core)
+        from_sibling(last)
+        finish(1 - core)
+    else:
+        lax.fori_loop(0, slots, slot, 0)
+        from_sibling(last)
+        lax.fori_loop(done(last), slots + chunks, lambda v, _: work(v), 0)
 
     def sent(s, way, count):
         ref = full.at[s, pl.ds(0, count * size)]
@@ -372,7 +402,8 @@
     size = rows // chunks
     length = n_col // 4
     ends = [*range(4), *range(n_col - 4, n_col)]
-    quick = length > 2 and all(trigger(n_row, n_col, chunks, size, tile, me) < chunks // 2 for me in ends)
+    whole = size % tile == 0 and tile % 16 == 0 and chunks % 4 == 0
+    quick = length > 2 and whole and all(trigger(n_row, n_col, chunks, size, tile, me) < chunks // 2 for me in ends)
     span = tile + tile % 16
     blocks = -(-tile // 128)
     gram = pl.pallas_call(

time: 163 us -> 162 us (level)
  no operation moved by 1% of the time
where the time goes in v4:
time: 162 us
  Pallas kernels  160 us (99%)
  local copies, waits for them, and re-layouts  2.2 us (1%)
    pallas_call x1, Pallas kernels, local(): pl.pallas_call(functools.partial(gather_gram, n_row, n_col, chunks, quick...  156 us
    pallas_call x1, Pallas kernels, local(): pl.pallas_call(functools.partial(flatten, tile, group, block), out_shape=...  4.31 us

profile of v4, /device:TPU:0, one launch (start us, length us, event | category | flops | bytes accessed | tf_op | source)
XLA Modules:
  0.0 162.1 jit_solution(7329482828908972144)
XLA Ops:
  0.0 0.0 copy-start
  0.0 1.5 copy-done
  1.5 0.0 copy-start.1
  1.5 0.7 copy-done.1
  2.2 155.6 %gather_gram.1.gram_ref = f32[4,3712,128]{2,1,0:T(8,128)S(1)} custom-call(bf16[3712,256]{1,0:T(8,128)(2,1)S(1)} %copy-done, f32[1,256]{1,0:T(1,128)S(1)} %bitcast.2), custom_call_target="tpu_custom_call" | custom-call | tf_op jit(solution)/shard_map/gather_gram/pallas_call | solution.py:409
  157.8 4.3 %flatten.1 = f32[13456,128]{1,0:T(8,128)} custom-call(f32[4,3712,128]{2,1,0:T(8,128)S(1)} %gather_gram.1.gram_ref), custom_call_target="tpu_custom_call" | custom-call | tf_op jit(solution)/shard_map/flatten/pallas_call | solution.py:436
Async XLA Ops:
  0.0 1.5 copy-start
  1.5 0.7 copy-start.1

commit v5 on v4

--- a/solution.py
+++ b/solution.py
@@ -8,8 +8,8 @@
 from jax.sharding import PartitionSpec as P
 
 MEMBERS = 7424
-MAX_CHUNKS = 8
-PIECES = 6
+MAX_CHUNKS = 4
+PIECE = 80
 MESH = pl.DeviceIdType.MESH
 
 
@@ -25,9 +25,10 @@
 
 
 def gather_gram(
-    n_row, n_col, chunks, quick, tile, x_ref, weight_ref, out_ref, full, cols, sums, recv, send, col_recv, col_send,
-    sum_recv, sum_send,
+    n_row, n_col, chunks, quick, tile, group, x_ref, weight_ref, out_ref, *rest,
 ):
+    half_ref = rest[0] if quick else None
+    full, cols, sums, recv, send, col_recv, col_send, sum_recv, sum_send = rest[1:] if quick else rest
     rows, depth = x_ref.shape
     length = n_col // 4
     size = rows // chunks
@@ -251,6 +252,12 @@
             late(m, 0)
             late(m, 1)
 
+        @pl.when(t == slots - 1)
+        def _():
+            groups = rows // group // 2
+            start = jnp.where(backward, groups, 0)
+            flatten_rows(tile, group, out_ref, start, groups, half_ref, 0)
+
         from_across(t)
         return now
 
@@ -365,33 +372,56 @@
         pltpu.make_async_copy(sums.at[i], sums.at[i], sum_send.at[n]).wait()
 
 
-def flatten(tile, group, block, gram_ref, flat_ref, buffer, sem):
+def flatten_rows(tile, group, gram_ref, start, many, flat_ref, to_row):
+    wide = group * tile // 128
+    scale = jnp.float32(1.0 / (MEMBERS - 1))
+    first = start * group if isinstance(start, int) else pl.multiple_of(start * group, group)
+    lane = lax.broadcasted_iota(jnp.int32, (many, 128), 1)
+    for s in range(wide):
+        value = None
+        at = s * 128
+        while at < (s + 1) * 128:
+            r, c, to = at // tile, at % tile, at - s * 128
+            count = min(tile - c, (s + 1) * 128 - at)
+            shift = (to - c) % 128
+            row = pl.ds(first + r, many, stride=group)
+            here = gram_ref[c // 128, row, :]
+            here = pltpu.roll(here, shift, 1) if shift else here
+            if c % 128 + count > 128:
+                then = gram_ref[c // 128 + 1, row, :]
+                then = pltpu.roll(then, shift, 1) if shift else then
+                here = jnp.where(lane < to + 128 - c % 128, here, then)
+            value = here if value is None else jnp.where(lane < to, value, here)
+            at += count
+        flat_ref[pl.ds(to_row + s, many, stride=wide), :] = value * scale
+
+
+def flatten(n_row, tile, group, gram_ref, *rest):
     groups = gram_ref.shape[1] // group
     wide = group * tile // 128
-    scale = jnp.float32(1.0 / (MEMBERS - 1))
-    for start in range(0, groups, block):
-        many = min(block, groups - start)
-        lane = lax.broadcasted_iota(jnp.int32, (many, 128), 1)
-        for s in range(wide):
-            value = None
-            at = s * 128
-            while at < (s + 1) * 128:
-                r, c, to = at // tile, at % tile, at - s * 128
-                count = min(tile - c, (s + 1) * 128 - at)
-                shift = (to - c) % 128
-                row = pl.ds(start * group + r, many, stride=group)
-                here = gram_ref[c // 128, row, :]
-                here = pltpu.roll(here, shift, 1) if shift else here
-                if c % 128 + count > 128:
-                    then = gram_ref[c // 128 + 1, row, :]
-                    then = pltpu.roll(then, shift, 1) if shift else then
-                    here = jnp.where(lane < to + 128 - c % 128, here, then)
-                value = here if value is None else jnp.where(lane < to, value, here)
-                at += count
-            buffer[pl.ds(start * wide + s, many, stride=wide), :] = value * scale
-        piece = pl.ds(start * wide, many * wide)
-        pltpu.make_async_copy(buffer.at[piece], flat_ref.at[piece], sem).start()
-    pltpu.make_async_copy(buffer, flat_ref, sem).wait()
+    if len(rest) == 5:
+        half_ref, flat_ref, buffer, sem, half_sem = rest
+        groups //= 2
+        backward = 2 * lax.axis_index("mrow") >= n_row
+        start, done = jnp.where(backward, 0, groups), jnp.where(backward, groups, 0)
+        half_copy = pltpu.make_async_copy(
+            half_ref, flat_ref.at[pl.ds(pl.multiple_of(done * wide, 8), groups * wide)], half_sem
+        )
+        half_copy.start()
+    else:
+        flat_ref, buffer, sem = rest
+        start, half_copy = 0, None
+    for piece in range(0, groups, PIECE):
+        many = min(PIECE, groups - piece)
+        flatten_rows(tile, group, gram_ref, start + piece, many, buffer, piece * wide)
+        target = (start + piece) * wide
+        target = target if half_copy is None else pl.multiple_of(target, 8)
+        pltpu.make_async_copy(
+            buffer.at[pl.ds(piece * wide, many * wide)], flat_ref.at[pl.ds(target, many * wide)], sem
+        ).start()
+    pltpu.make_async_copy(buffer, flat_ref.at[pl.ds(0, groups * wide)], sem).wait()
+    if half_copy is not None:
+        half_copy.wait()
 
 
 def local(n_row, n_col, snapshots, area_weight):
@@ -406,11 +436,18 @@
     quick = length > 2 and whole and all(trigger(n_row, n_col, chunks, size, tile, me) < chunks // 2 for me in ends)
     span = tile + tile % 16
     blocks = -(-tile // 128)
-    gram = pl.pallas_call(
-        functools.partial(gather_gram, n_row, n_col, chunks, quick, tile),
-        out_shape=jax.ShapeDtypeStruct((blocks, rows, 128), jnp.float32),
+    group = 8
+    while group * tile % 128:
+        group *= 2
+    flat_shape = (rows * tile // 128, 128)
+    half_shape = (flat_shape[0] // 2, 128)
+    quick = quick and rows % (16 * group) == 0 and half_shape[0] % 8 == 0
+    shapes = [(blocks, rows, 128)] + [half_shape] * quick
+    parts = pl.pallas_call(
+        functools.partial(gather_gram, n_row, n_col, chunks, quick, tile, group),
+        out_shape=[jax.ShapeDtypeStruct(shape, jnp.float32) for shape in shapes],
         in_specs=[pl.BlockSpec(memory_space=pltpu.VMEM)] * 2,
-        out_specs=pl.BlockSpec(memory_space=pltpu.VMEM),
+        out_specs=[pl.BlockSpec(memory_space=pltpu.VMEM)] * len(shapes),
         scratch_shapes=[
             pltpu.VMEM((n_col, rows, depth), jnp.bfloat16),
             pltpu.VMEM((n_col, span, depth), jnp.bfloat16),
@@ -423,25 +460,22 @@
             pltpu.SemaphoreType.DMA((max(n_row - 1, 1),)),
         ],
         compiler_params=pltpu.CompilerParams(
-            collective_id=0, has_side_effects=True, vmem_limit_bytes=44 * 2**20
+            collective_id=0, has_side_effects=True, vmem_limit_bytes=38 * 2**20
         ),
         name="gather_gram",
     )(snapshots, area_weight.reshape(1, depth))
-    group = 8
-    while group * tile % 128:
-        group *= 2
-    groups = rows // group
-    block = (groups // PIECES + 7) // 8 * 8
-    flat_shape = (groups * group * tile // 128, 128)
     flat = pl.pallas_call(
-        functools.partial(flatten, tile, group, block),
+        functools.partial(flatten, n_row, tile, group),
         out_shape=jax.ShapeDtypeStruct(flat_shape, jnp.float32),
-        in_specs=[pl.BlockSpec(memory_space=pltpu.VMEM)],
+        in_specs=[pl.BlockSpec(memory_space=pltpu.VMEM)] * len(shapes),
         out_specs=pl.BlockSpec(memory_space=pl.ANY),
-        scratch_shapes=[pltpu.VMEM(flat_shape, jnp.float32), pltpu.SemaphoreType.DMA],
-        compiler_params=pltpu.CompilerParams(vmem_limit_bytes=24 * 2**20),
+        scratch_shapes=[
+            pltpu.VMEM(half_shape if quick else flat_shape, jnp.float32),
+            *[pltpu.SemaphoreType.DMA] * len(shapes),
+        ],
+        compiler_params=pltpu.CompilerParams(vmem_limit_bytes=16 * 2**20),
         name="flatten",
-    )(gram)
+    )(*parts)
     return flat.reshape(1, 1, rows * tile)
 
 

time: 162 us -> 160 us (0.988)
  Pallas kernels: 160 us -> 157 us
where the time goes in v5:
time: 160 us
  Pallas kernels  157 us (98%)
  local copies, waits for them, and re-layouts  2.2 us (1%)
    pallas_call x1, Pallas kernels, local(): pl.pallas_call(functools.partial(gather_gram, n_row, n_col, chunks, quick...  155 us

profile of v5, /device:TPU:0, one launch (start us, length us, event | category | flops | bytes accessed | tf_op | source)
XLA Modules:
  0.0 159.7 jit_solution(10654188057518786693)
XLA Ops:
  0.0 0.0 copy-start
  0.0 1.5 copy-done
  1.5 0.0 copy-start.1
  1.5 0.7 copy-done.1
  2.2 154.6 %gather_gram.1 = (f32[4,3712,128]{2,1,0:T(8,128)S(1)}, f32[6728,128]{1,0:T(8,128)S(1)}) custom-call(bf16[3712,256]{1,0:T(8,128)(2,1)S(1)} %copy-done, f32[1,256]{1,0:T(1,128)S(1)} %bitcast.2), custom_call_target="tpu_custom_call" | custom-call | tf_op jit(solution)/shard_map/gather_gram/pallas_call | solution.py:446
  156.8 2.9 %flatten.1 = f32[13456,128]{1,0:T(8,128)} custom-call(f32[4,3712,128]{2,1,0:T(8,128)S(1)} %get-tuple-element.7.gram_ref, f32[6728,128]{1,0:T(8,128)S(1)} %get-tuple-element.8.rest_0_), custom_call_target="tpu_custom_call" | custom-call | tf_op jit(solution)/shard_map/flatten/pallas_call | solution.py:467
Async XLA Ops:
  0.0 1.5 copy-start
  1.5 0.7 copy-start.1

commit v6 on v5

--- a/solution.py
+++ b/solution.py
@@ -7,7 +7,6 @@
 from jax.experimental.pallas import tpu as pltpu
 from jax.sharding import PartitionSpec as P
 
-MEMBERS = 7424
 MAX_CHUNKS = 4
 PIECE = 80
 MESH = pl.DeviceIdType.MESH
@@ -139,7 +138,7 @@
     out_ref[...] = jnp.zeros_like(out_ref)
     for peer in peers:
         pltpu.make_async_copy(sums.at[peer], sums.at[peer], sum_recv.at[peer]).wait()
-    mean = jnp.sum(jnp.sum(sums[...], axis=0), axis=0, keepdims=True) / MEMBERS
+    mean = jnp.sum(jnp.sum(sums[...], axis=0), axis=0, keepdims=True) / (rows * n_row)
     root_weight = jnp.sqrt(weight_ref[...])
 
     def center(k):
@@ -256,7 +255,7 @@
         def _():
             groups = rows // group // 2
             start = jnp.where(backward, groups, 0)
-            flatten_rows(tile, group, out_ref, start, groups, half_ref, 0)
+            flatten_rows(rows * n_row, tile, group, out_ref, start, groups, half_ref, 0)
 
         from_across(t)
         return now
@@ -372,9 +371,9 @@
         pltpu.make_async_copy(sums.at[i], sums.at[i], sum_send.at[n]).wait()
 
 
-def flatten_rows(tile, group, gram_ref, start, many, flat_ref, to_row):
+def flatten_rows(members, tile, group, gram_ref, start, many, flat_ref, to_row):
     wide = group * tile // 128
-    scale = jnp.float32(1.0 / (MEMBERS - 1))
+    scale = jnp.float32(1.0 / (members - 1))
     first = start * group if isinstance(start, int) else pl.multiple_of(start * group, group)
     lane = lax.broadcasted_iota(jnp.int32, (many, 128), 1)
     for s in range(wide):
@@ -397,6 +396,7 @@
 
 
 def flatten(n_row, tile, group, gram_ref, *rest):
+    members = gram_ref.shape[1] * n_row
     groups = gram_ref.shape[1] // group
     wide = group * tile // 128
     if len(rest) == 5:
@@ -413,7 +413,7 @@
         start, half_copy = 0, None
     for piece in range(0, groups, PIECE):
         many = min(PIECE, groups - piece)
-        flatten_rows(tile, group, gram_ref, start + piece, many, buffer, piece * wide)
+        flatten_rows(members, tile, group, gram_ref, start + piece, many, buffer, piece * wide)
         target = (start + piece) * wide
         target = target if half_copy is None else pl.multiple_of(target, 8)
         pltpu.make_async_copy(

time: 160 us -> 160 us (level)
  no operation moved by 1% of the time
where the time goes in v6:
time: 160 us
  Pallas kernels  157 us (98%)
  local copies, waits for them, and re-layouts  2.2 us (1%)
    pallas_call x1, Pallas kernels, local(): pl.pallas_call(functools.partial(gather_gram, n_row, n_col, chunks, quick...  155 us

profile of v6, /device:TPU:0, one launch (start us, length us, event | category | flops | bytes accessed | tf_op | source)
XLA Modules:
  0.0 159.7 jit_solution(10654188057518786693)
XLA Ops:
  0.0 0.0 copy-start
  0.0 1.5 copy-done
  1.5 0.0 copy-start.1
  1.5 0.7 copy-done.1
  2.2 154.6 %gather_gram.1 = (f32[4,3712,128]{2,1,0:T(8,128)S(1)}, f32[6728,128]{1,0:T(8,128)S(1)}) custom-call(bf16[3712,256]{1,0:T(8,128)(2,1)S(1)} %copy-done, f32[1,256]{1,0:T(1,128)S(1)} %bitcast.2), custom_call_target="tpu_custom_call" | custom-call | tf_op jit(solution)/shard_map/gather_gram/pallas_call | solution.py:446
  156.8 2.9 %flatten.1 = f32[13456,128]{1,0:T(8,128)} custom-call(f32[4,3712,128]{2,1,0:T(8,128)S(1)} %get-tuple-element.7.gram_ref, f32[6728,128]{1,0:T(8,128)S(1)} %get-tuple-element.8.rest_0_), custom_call_target="tpu_custom_call" | custom-call | tf_op jit(solution)/shard_map/flatten/pallas_call | solution.py:467
Async XLA Ops:
  0.0 1.5 copy-start
  1.5 0.7 copy-start.1

commit v7 on v6

--- a/solution.py
+++ b/solution.py
@@ -269,13 +269,19 @@
         def _():
             pltpu.make_async_copy(cols.at[s], cols.at[s], col_recv.at[s]).wait()
 
-    def add_product(s, k):
-        row = rows_of(s, k)
+    def columns(s):
         right = cols[s]
         if span != tile:
             right = jnp.where(offset == aligned, right[:tile], right[span - tile:])
-        product = lax.dot_general(
-            full[s, row, :], right, (((1,), (1,)), ((), ())), preferred_element_type=jnp.float32
+        return right
+
+    def add_product(sources, k):
+        row = rows_of(sources[0], k)
+        product = sum(
+            lax.dot_general(
+                full[s, row, :], columns(s), (((1,), (1,)), ((), ())), preferred_element_type=jnp.float32
+            )
+            for s in sources
         )
         for b in range(out_ref.shape[0]):
             width = min(128, tile - b * 128)
@@ -300,7 +306,7 @@
             def _():
                 s = index(place, lax.rem(side + cross, 2), lax.rem(n, 2))
                 pl.when(k == 0)(lambda: take_cols(s))
-                add_product(s, k)
+                add_product([s], k)
 
             return 0
 
@@ -308,7 +314,7 @@
         return 0
 
     def late(k, lane):
-        add_product(index(near, 1 - side, lane), k)
+        add_product([index(near, 1 - side, lane)], k)
 
     def ready_own(k, _):
         s = index(line, side, 1 - core)
@@ -323,8 +329,12 @@
         lax.fori_loop(final, slots, end_slot, done(jnp.int32(final - 1)))
 
         def finish(lane):
-            work(last + chunks, lane)
-            pl.when(end)(lambda: late(chunks - 1, lane))
+            @pl.when(jnp.logical_not(end))
+            def _():
+                work(last + chunks, lane)
+
+            far = index(jnp.where(line == 0, length - 1, 0), 1 - side, lane)
+            pl.when(end)(lambda: add_product([far, index(near, 1 - side, lane)], chunks - 1))
 
         finish(core)
         from_sibling(last)

time: 160 us -> 160 us (level)
  no operation moved by 1% of the time
where the time goes in v7:
time: 160 us; the launch traced here: 159 us
  Pallas kernels  157 us (98%)
  local copies, waits for them, and re-layouts  2.2 us (1%)
    pallas_call x1, Pallas kernels, local(): pl.pallas_call(functools.partial(gather_gram, n_row, n_col, chunks, quick...  154 us

profile of v7, /device:TPU:0, one launch (start us, length us, event | category | flops | bytes accessed | tf_op | source)
XLA Modules:
  0.0 159.4 jit_solution(3500679730708774015)
XLA Ops:
  0.0 0.0 copy-start
  0.0 1.5 copy-done
  1.5 0.0 copy-start.1
  1.5 0.7 copy-done.1
  2.2 154.3 %gather_gram.1 = (f32[4,3712,128]{2,1,0:T(8,128)S(1)}, f32[6728,128]{1,0:T(8,128)S(1)}) custom-call(bf16[3712,256]{1,0:T(8,128)(2,1)S(1)} %copy-done, f32[1,256]{1,0:T(1,128)S(1)} %bitcast.2), custom_call_target="tpu_custom_call" | custom-call | tf_op jit(solution)/shard_map/gather_gram/pallas_call | solution.py:456
  156.5 2.9 %flatten.1 = f32[13456,128]{1,0:T(8,128)} custom-call(f32[4,3712,128]{2,1,0:T(8,128)S(1)} %get-tuple-element.7.gram_ref, f32[6728,128]{1,0:T(8,128)S(1)} %get-tuple-element.8.rest_0_), custom_call_target="tpu_custom_call" | custom-call | tf_op jit(solution)/shard_map/flatten/pallas_call | solution.py:477
Async XLA Ops:
  0.0 1.5 copy-start
  1.5 0.7 copy-start.1
